TPU v7x, 32 devices: a whole 2x2x4 slice. The times are simulated.
32 devices in a mesh: seq: 8 (over z, x), head: 4 (over y, core).
Axes of the slice: x: 2, y: 2, z: 4, core: 2. Of those that a mesh axis runs over, the one named last changes fastest.
Arguments:
- tokens: bfloat16 [2048, 3584], P('seq'), may hold values from -16 to 16
- length: int32 [1], replicated, may hold values from 512 to 2048
- in_gain: float32 [3584], replicated, may hold values from 0.5 to 1.5
- q_weight: bfloat16 [3584, 3584], P(None, 'head'), may hold values from -0.09375 to 0.09375
- q_bias: float32 [3584], P('head'), may hold values from -60 to 60
- k_weight: bfloat16 [3584, 512], P(None, 'head'), may hold values from -0.09375 to 0.09375
- k_bias: float32 [512], P('head'), may hold values from -60 to 60
- v_weight: bfloat16 [3584, 512], P(None, 'head'), may hold values from -0.09375 to 0.09375
- v_bias: float32 [512], P('head'), may hold values from -2 to 2
- o_weight: bfloat16 [3584, 3584], P('head'), may hold values from -0.125 to 0.125
- final_gain: float32 [3584], P('head'), may hold values from 0.5 to 1.5
Outputs:
- hidden: bfloat16 [2048, 3584], P('seq', 'head')
- embedding: float32 [3584], P('head')
All inputs are finite; a program needn't handle non-finite values.
Results may differ from a plain program's by a relative error of at most 0.0075.
The roundings to bfloat16 on the way count: a program that leaves them out, or rounds other values in their place, can miss the bound.
Values may be sent and summed in bfloat16 or wider, within the bound.
A program may use at most 192 MiB of HBM per device.

v0:
```python
import jax
import jax.numpy as jnp
from jax import lax
from jax.sharding import PartitionSpec as P

D = 3584
HEAD_DIM = 128
rope_base = 1000000.0
epsilon = 1e-06


def rms_norm(inputs, gain):
    inputs = inputs.astype(jnp.float32)
    return inputs * lax.rsqrt(jnp.mean(inputs * inputs, axis=-1, keepdims=True) + epsilon) * gain


def rope_tables(positions):
    half_dim = HEAD_DIM // 2
    inverse = rope_base ** (-(jnp.arange(half_dim, dtype=jnp.float32) * 2.0) / HEAD_DIM)
    angles = positions.astype(jnp.float32)[:, None] * inverse[None, :]
    angles = jnp.concatenate([angles, angles], axis=1)
    return (jnp.cos(angles), jnp.sin(angles))


def rotate(inputs, cosine, sine):
    half_dim = HEAD_DIM // 2
    turned = jnp.concatenate([-inputs[..., half_dim:], inputs[..., :half_dim]], axis=-1)
    return inputs * cosine[:, None, :] + turned * sine[:, None, :]


def key_scores(queries, key_block):
    return lax.dot_general(
        queries, key_block, (((1,), (1,)), ((), ())), preferred_element_type=jnp.float32
    )


def body(
    tokens,
    length,
    in_gain,
    q_weight,
    q_bias,
    k_weight,
    k_bias,
    v_weight,
    v_bias,
    o_weight,
    final_gain,
):
    tok_rows = tokens.shape[0]
    head_count = q_weight.shape[1] // HEAD_DIM
    offset = lax.axis_index("seq") * tok_rows
    limit = length[0]
    positions = offset + jnp.arange(tok_rows, dtype=jnp.int32)
    normed = rms_norm(tokens, in_gain).astype(jnp.bfloat16)
    cosine, sine = rope_tables(positions)
    query = jnp.dot(normed, q_weight, preferred_element_type=jnp.float32) + q_bias
    query = rotate(query.reshape(tok_rows, head_count, HEAD_DIM), cosine, sine) * HEAD_DIM ** (-0.5)
    query = query.astype(jnp.bfloat16).reshape(tok_rows * head_count, HEAD_DIM)
    keys = jnp.dot(normed, k_weight, preferred_element_type=jnp.float32) + k_bias
    keys = (
        rotate(keys.reshape(tok_rows, 1, HEAD_DIM), cosine, sine)
        .astype(jnp.bfloat16)
        .reshape(tok_rows, HEAD_DIM)
    )
    values = (jnp.dot(normed, v_weight, preferred_element_type=jnp.float32) + v_bias).astype(
        jnp.bfloat16
    )
    q_rows = query.shape[0]

    def absorb(carry, piece):
        top, total, accum = carry
        k_piece, v_piece = piece
        count = k_piece.shape[0]
        live = jnp.arange(count, dtype=jnp.int32) < limit
        scores = jnp.where(live[None, :], key_scores(query, k_piece), -1e30)
        new_top = jnp.maximum(top, jnp.max(scores, axis=1))
        weights = jnp.where(live[None, :], jnp.exp(scores - new_top[:, None]), 0.0)
        total = jnp.sum(weights, axis=1)
        accum = jnp.dot(weights.astype(jnp.bfloat16), v_piece, preferred_element_type=jnp.float32)
        return (new_top, total, accum)

    initial = (
        jnp.full((q_rows,), -1e30, jnp.float32),
        jnp.zeros((q_rows,), jnp.float32),
        jnp.zeros((q_rows, HEAD_DIM), jnp.float32),
    )
    piece = (
        lax.all_gather(keys, "seq", axis=0, tiled=True),
        lax.all_gather(values, "seq", axis=0, tiled=True),
    )

    def update(state):
        return absorb(state, piece)

    def unchanged(state):
        return state

    top, total, accum = lax.cond(jnp.int32(0) < limit, update, unchanged, initial)
    attended = (
        (accum / total[:, None]).astype(jnp.bfloat16).reshape(tok_rows, head_count * HEAD_DIM)
    )
    mixed = jnp.dot(attended, o_weight, preferred_element_type=jnp.float32)
    width_share = D // lax.axis_size("head")
    column = lax.axis_index("head") * width_share
    shared = lax.psum_scatter(
        mixed.astype(jnp.bfloat16), "head", scatter_dimension=1, tiled=True
    ).astype(jnp.float32)
    hidden_full = (
        lax.dynamic_slice_in_dim(tokens, column, width_share, 1).astype(jnp.float32) + shared
    )
    squares = lax.psum(jnp.sum(hidden_full * hidden_full, axis=1), "head")
    final = hidden_full * lax.rsqrt(squares[:, None] / D + epsilon) * final_gain
    row_live = positions < limit
    local_sum = jnp.sum(jnp.where(row_live[:, None], final, 0.0), axis=0)
    pooled_sum = lax.psum(local_sum, "seq")
    mean = pooled_sum / limit.astype(jnp.float32)
    power = lax.psum(jnp.sum(mean * mean), "head")
    embedding = mean * lax.rsqrt(power / D + epsilon)
    return (hidden_full.astype(jnp.bfloat16), embedding)


def solution(mesh):
    in_specs = (
        P("seq", None),
        P(),
        P(),
        P(None, "head"),
        P("head"),
        P(None, "head"),
        P("head"),
        P(None, "head"),
        P("head"),
        P("head", None),
        P("head"),
    )
    out_specs = (P("seq", "head"), P("head"))
    return jax.shard_map(body, mesh=mesh, in_specs=in_specs, out_specs=out_specs, check_vma=False)
```

profile of v0, /device:TPU:0, one launch (start us, length us, event | category | flops | bytes accessed | tf_op | source)
XLA Modules:
  0.0 211.3 jit_solution(12068621012374544557)
XLA Ops:
  7.2 0.0 copy-start
  7.2 0.0 reduce-scatter.4.cloned.1.call-start
  7.2 2.0 fusion.7
  9.3 6.5 %convolution_add_fusion = f32[256,896]{1,0:T(8,128)} fusion(bf16[3584,896]{1,0:T(8,128)(2,1)} %param.16, f32[896]{0:T(1024)} %param.17, bf16[256,3584]{1,0:T(8,128)(2,1)} %param.13, f32[3584]{0:T(1024)} %param.15, f32[256]{0:T(256)S(1)} %add_rsqrt_fusion.1), kind=kOutput, calls=%fused_computation.16 | convolution fusion | flops 1648066560 | bytes 9193984 | tf_op jit(solution)/shard_map/dot_general | solution.py:57
  15.7 2.6 %copy.23 = f32[256,896]{0,1:T(8,128)} copy(f32[256,896]{1,0:T(8,128)} %convolution_add_fusion) | data formatting | bytes 1835008 | tf_op jit(solution)/shard_map/add | solution.py:57
  18.3 2.2 %reshape.119 = f32[1792,128]{1,0:T(8,128)} reshape(f32[256,896]{1,0:T(8,128)} %convolution_add_fusion) | data formatting | bytes 1835008 | tf_op jit(solution)/shard_map/reshape | solution.py:58
  21.2 0.0 copy-done
  21.2 0.0 copy-done.1
  21.2 0.0 copy-done.7
  21.2 0.0 copy-done.8
  21.2 0.9 convolution_add_fusion.2
  22.1 0.1 broadcast_multiply_fusion
  22.2 1.1 fusion.18
  23.3 0.1 copy.26
  23.4 0.1 copy.22
  23.5 0.0 copy-start.4
  23.5 33.5 %all_gather.6 = bf16[2048,128]{0,1:T(8,128)(2,1)S(1)} all-gather(bf16[256,128]{0,1:T(8,128)(2,1)} %get-tuple-element.38), channel_id=1, replica_groups=mesh['seq'=8,'head'=4] {'seq'}, dimensions={0}, use_global_device_ids=true | all-gather | bytes 589824 | tf_op jit(solution)/shard_map/all_gather | solution.py:89
  57.0 1.9 fusion.10
  58.9 33.4 %all_gather.7 = bf16[2048,128]{1,0:T(8,128)(2,1)} all-gather(bf16[256,128]{1,0:T(8,128)(2,1)S(1)} %fusion.10), channel_id=1, replica_groups=mesh['seq'=8,'head'=4] {'seq'}, dimensions={0}, use_global_device_ids=true | all-gather | bytes 589824 | tf_op jit(solution)/shard_map/all_gather | solution.py:90
  92.3 0.9 slice_negate_fusion
  93.1 0.4 copy.24
  93.6 1.0 concatenate.28
  94.6 0.1 mul.130
  94.7 1.0 mul.131
  95.7 0.1 mul.133
  95.8 1.1 mul.134
  96.8 1.4 copy.25
  98.3 1.0 concatenate.29
  99.3 2.4 %fusion.13 = bf16[1792,128]{1,0:T(8,128)(2,1)S(1)} fusion(f32[1792,128]{1,0:T(8,128)} %mul.134, f32[1792,64]{1,0:T(8,128)} %concatenate.29, f32[1792,64]{1,0:T(8,128)} %concatenate.28, f32[1792,128]{1,0:T(8,128)S(1)} %copy-done.3, f32[1792,128]{1,0:T(8,128)} %mul.131), kind=kLoop, calls=%fused_computation.23 | loop fusion | flops 1376256 | bytes 4128768 | tf_op jit(solution)/shard_map/convert_element_type | solution.py:59
  101.7 22.9 %conditional.1 = (f32[1792]{0:T(1024)S(1)}, f32[1792,128]{1,0:T(8,128)S(1)}) conditional(s32[]{:T(128)} %convert_element_type.49, () %tuple.16, (s32[]{:T(128)}, bf16[1792,128]{1,0:T(8,128)(2,1)S(1)}, bf16[2048,128]{0,1:T(8,128)(2,1)S(1)}, bf16[2048,128]{1,0:T(8,128)(2,1)S(1)}) %tuple.32), branch_computations={%region_1.0_spmd, %region_2.5_spmd} | conditional | flops 1915748608 | bytes 46516244 | solution.py:99
  101.9 0.7 iota_compare_fusion
  102.6 7.3 %select_reduce_fusion = (f32[1792]{0:T(1024)S(1)}, f32[1792,2048]{1,0:T(8,128)}) fusion(pred[2048]{0:T(1024)(128)(4,1)S(1)} %iota_compare_fusion, bf16[1792,128]{1,0:T(8,128)(2,1)S(1)} %get-tuple-element.9, bf16[2048,128]{0,1:T(8,128)(2,1)S(1)} %get-tuple-element.28), kind=kOutput, calls=%fused_computation.1 | convolution fusion | flops 946862336 | bytes 15672320 | tf_op jit(solution)/shard_map/cond/branch_1_fun/dot_general | solution.py:32
  109.9 8.2 %fusion.1 = f32[1792]{0:T(1024)S(1)} fusion(f32[1792,2048]{1,0:T(8,128)} %get-tuple-element.31, f32[1792]{0:T(1024)S(1)} %broadcast_maximum_fusion, pred[2048]{0:T(1024)(128)(4,1)S(1)} %iota_compare_fusion), kind=kLoop, calls=%fused_computation.3 | loop fusion | flops 14678272 | bytes 14696448 | tf_op jit(solution)/shard_map/cond/branch_1_fun/reduce_sum | solution.py:79
  118.0 6.6 %fusion.2 = f32[1792,128]{1,0:T(8,128)S(1)} fusion(bf16[2048,128]{1,0:T(8,128)(2,1)S(1)} %get-tuple-element.11, f32[1792,2048]{1,0:T(8,128)} %get-tuple-element.31, f32[1792]{0:T(1024)S(1)} %broadcast_maximum_fusion, pred[2048]{0:T(1024)(128)(4,1)S(1)} %iota_compare_fusion), kind=kOutput, calls=%fused_computation.4 | convolution fusion | flops 954204160 | bytes 16131072 | tf_op jit(solution)/shard_map/cond/branch_1_fun/dot_general | solution.py:80
  124.6 0.3 divide_convert_fusion
  125.0 0.5 reshape.122
  125.4 6.1 %convolution_convert_fusion = bf16[256,3584]{1,0:T(8,128)(2,1)} fusion(bf16[256,896]{1,0:T(8,128)(2,1)S(1)} %reshape.122, bf16[896,3584]{1,0:T(8,128)(2,1)} %param.22), kind=kOutput, calls=%fused_computation.10 | convolution fusion | flops 1645084672 | bytes 8716288 | tf_op jit(solution)/shard_map/dot_general | solution.py:103
  131.6 4.0 %copy.29 = bf16[256,3584]{0,1:T(8,128)(2,1)} copy(bf16[256,3584]{1,0:T(8,128)(2,1)} %convolution_convert_fusion) | data formatting | bytes 3670016
  135.5 0.0 reduce-scatter.4.cloned.1.call-update
  135.6 30.9 %reduce-scatter.4.cloned.1.call-done = bf16[896,256]{1,0:T(8,128)(2,1)} async-done(((bf16[3584,256]{1,0:T(8,128)(2,1)}), bf16[896,256]{1,0:T(8,128)(2,1)}) %reduce-scatter.4.cloned.1.call-update) | async-done | bytes 458768
  166.5 1.3 copy.30
  167.8 0.2 multiply_reduce_fusion
  168.0 5.8 %psum.21 = f32[256]{0:T(256)S(1)} all-reduce(f32[256]{0:T(256)S(1)} %multiply_reduce_fusion), channel_id=1, replica_groups=mesh['seq'=8,'head'=4] {'head'}, use_global_device_ids=true, to_apply=%region_7.8 | all-reduce | flops 256 | bytes 2048 | tf_op jit(solution)/shard_map/psum | solution.py:112
  173.8 1.0 select_reduce_fusion.1
  174.8 21.5 %psum.22 = f32[896]{0:T(1024)S(1)} all-reduce(f32[896]{0:T(1024)S(1)} %get-tuple-element.32), channel_id=1, replica_groups=mesh['seq'=8,'head'=4] {'seq'}, use_global_device_ids=true, to_apply=%region_9.10 | all-reduce | flops 896 | bytes 7168 | tf_op jit(solution)/shard_map/psum | solution.py:116
  196.3 0.6 multiply_reduce_fusion.1
  196.9 6.3 %psum.23 = f32[]{:T(128)} all-reduce(f32[]{:T(128)} %multiply_reduce_fusion.1), channel_id=1, replica_groups=mesh['seq'=8,'head'=4] {'head'}, use_global_device_ids=true, to_apply=%region_11.12 | all-reduce | flops 1 | bytes 8 | tf_op jit(solution)/shard_map/psum | solution.py:118
  203.9 0.6 broadcast_multiply_fusion.1
  (21 shorter events, 0.1 us)
Async XLA Ops:
  7.2 14.0 %copy-start = (bf16[3584,128]{1,0:T(8,128)(2,1)S(1)}, bf16[3584,128]{1,0:T(8,128)(2,1)}, u32[]{:S(2)}) copy-start(bf16[3584,128]{1,0:T(8,128)(2,1)} %param.18) | copy-start | bytes 2752516
  7.2 159.3 %reduce-scatter.4.cloned.1.call-start = ((), (), s32[]{:S(2)}) async-start(), calls=%async_computation.1 | async-start | bytes 2293760
  15.7 5.4 %copy-start.1 = (bf16[256,3584]{1,0:T(8,128)(2,1)S(1)}, bf16[256,3584]{1,0:T(8,128)(2,1)}, u32[]{:S(2)}) copy-start(bf16[256,3584]{1,0:T(8,128)(2,1)} %param.13) | copy-start | bytes 5505028
  15.7 5.5 %copy-start.7 = (f32[3584]{0:T(1024)S(1)}, f32[3584]{0:T(1024)}, u32[]{:S(2)}) copy-start(f32[3584]{0:T(1024)} %param.15) | copy-start | bytes 43012
  15.7 5.5 %copy-start.8 = (f32[128]{0:T(128)S(1)}, f32[128]{0:T(128)}, u32[]{:S(2)}) copy-start(f32[128]{0:T(128)} %param.19) | copy-start | bytes 1540
  18.3 38.7 %copy-start.9 = (f32[128]{0:T(128)S(1)}, f32[128]{0:T(128)}, u32[]{:S(2)}) copy-start(f32[128]{0:T(128)} %param.21) | copy-start | bytes 1540
  23.5 68.8 %copy-start.4 = (f32[256,896]{0,1:T(8,128)S(1)}, f32[256,896]{0,1:T(8,128)}, u32[]{:S(2)}) copy-start(f32[256,896]{0,1:T(8,128)} %copy.23) | copy-start | bytes 2752516
  95.7 3.6 %copy-start.3 = (f32[1792,128]{1,0:T(8,128)S(1)}, f32[1792,128]{1,0:T(8,128)}, u32[]{:S(2)}) copy-start(f32[1792,128]{1,0:T(8,128)} %reshape.119) | copy-start | bytes 2752516
  99.3 2.4 %copy-start.5 = (bf16[2048,128]{1,0:T(8,128)(2,1)S(1)}, bf16[2048,128]{1,0:T(8,128)(2,1)}, u32[]{:S(2)}) copy-start(bf16[2048,128]{1,0:T(8,128)(2,1)} %all_gather.7) | copy-start | bytes 1572868
  131.6 36.2 %copy-start.2 = (bf16[256,3584]{1,0:T(8,128)(2,1)S(1)}, bf16[256,3584]{1,0:T(8,128)(2,1)}, u32[]{:S(2)}) copy-start(bf16[256,3584]{1,0:T(8,128)(2,1)} %param.13) | copy-start | bytes 5505028
  131.6 42.2 %copy-start.6 = (f32[896]{0:T(1024)S(1)}, f32[896]{0:T(1024)}, u32[]{:S(2)}) copy-start(f32[896]{0:T(1024)} %param.23) | copy-start | bytes 10756
Sparse Core Ops, SparseCore 0:
  135.7 30.7 reduce-scatter.3
where the time goes:
time: 212 us; the launch traced here: 211 us
  blocking collectives  100 us (47%)
  waiting for transfers between devices  30.9 us (15%)
  matrix products  29.3 us (14%)
  other arithmetic  18.1 us (9%)
  local copies, waits for them, and re-layouts  16.8 us (8%)
  between operations  15.6 us (7%)
    all_gather x1, blocking collectives, body(): lax.all_gather(keys, 'seq', axis=0, tiled=True)  33.5 us
    all_gather x1, blocking collectives, body(): lax.all_gather(values, 'seq', axis=0, tiled=True)  33.4 us
    unnamed x2, waiting for transfers between devices  30.9 us
    psum x1, blocking collectives, body(): pooled_sum = lax.psum(local_sum, 'seq')  21.5 us
    reduce_sum x1, other arithmetic, absorb(): total = jnp.sum(weights, axis=1)  8.15 us
    dot_general x1, matrix products, key_scores(): lax.dot_general(queries, key_block, (((1,), (1,)), ((), ())), preferred_e...  7.28 us
    dot_general x1, matrix products, absorb(): jnp.dot(weights.astype(jnp.bfloat16), v_piece, preferred_element_type=jnp...  6.61 us
    dot_general x1, matrix products, body(): jnp.dot(normed, q_weight, preferred_element_type=jnp.float32) + q_bias  6.46 us
  transfers between devices with their start and end apart: 1, of which 1 were waited for; matrix products, arithmetic and copies ran while one was open for 0% of the time, Pallas kernels for 0%

commit v1 on v0

--- a/solution.py
+++ b/solution.py
@@ -113,7 +113,7 @@
     final = hidden_full * lax.rsqrt(squares[:, None] / D + epsilon) * final_gain
     row_live = positions < limit
     local_sum = jnp.sum(jnp.where(row_live[:, None], final, 0.0), axis=0)
-    pooled_sum = lax.psum(local_sum, "seq")
+    pooled_sum = jnp.sum(lax.all_gather(local_sum, "seq"), axis=0)
     mean = pooled_sum / limit.astype(jnp.float32)
     power = lax.psum(jnp.sum(mean * mean), "head")
     embedding = mean * lax.rsqrt(power / D + epsilon)

time: 212 us -> 221 us (1.042)
  blocking collectives: 100 us -> 110 us
    all_gather x0 -> x1, blocking collectives: none -> 30.8 us  [body(): pooled_sum = jnp.sum(lax.all_gather(local_sum, 'seq'), axis=0)]
    psum x1 -> x0, blocking collectives: 21.5 us -> none  [body(): pooled_sum = lax.psum(local_sum, 'seq')]
    unnamed x22 -> x23, local copies, waits for them, and re-layouts: 5.26 us -> 5.27 us
where the time goes in v1:
time: 221 us
  blocking collectives  110 us (50%)
  waiting for transfers between devices  30.9 us (14%)
  matrix products  29.3 us (13%)
  other arithmetic  18.1 us (8%)
  local copies, waits for them, and re-layouts  16.8 us (8%)
  between operations  15.6 us (7%)
    all_gather x1, blocking collectives, body(): lax.all_gather(keys, 'seq', axis=0, tiled=True)  33.5 us
    all_gather x1, blocking collectives, body(): lax.all_gather(values, 'seq', axis=0, tiled=True)  33.4 us
    unnamed x2, waiting for transfers between devices  30.9 us
    all_gather x1, blocking collectives, body(): pooled_sum = jnp.sum(lax.all_gather(local_sum, 'seq'), axis=0)  30.8 us
    reduce_sum x1, other arithmetic, absorb(): total = jnp.sum(weights, axis=1)  8.15 us
    dot_general x1, matrix products, key_scores(): lax.dot_general(queries, key_block, (((1,), (1,)), ((), ())), preferred_e...  7.28 us
    dot_general x1, matrix products, absorb(): jnp.dot(weights.astype(jnp.bfloat16), v_piece, preferred_element_type=jnp...  6.61 us
    dot_general x1, matrix products, body(): jnp.dot(normed, q_weight, preferred_element_type=jnp.float32) + q_bias  6.46 us
  transfers between devices with their start and end apart: 1, of which 1 were waited for; matrix products, arithmetic and copies ran while one was open for 0% of the time, Pallas kernels for 0%

profile of v1, /device:TPU:0, one launch (start us, length us, event | category | flops | bytes accessed | tf_op | source)
XLA Modules:
  0.0 220.7 jit_solution(11962654678633053908)
XLA Ops:
  7.2 0.0 copy-start
  7.2 0.0 reduce-scatter.4.cloned.1.call-start
  7.2 2.0 fusion.7
  9.3 6.5 %convolution_add_fusion = f32[256,896]{1,0:T(8,128)} fusion(bf16[3584,896]{1,0:T(8,128)(2,1)} %param.16, f32[896]{0:T(1024)} %param.17, bf16[256,3584]{1,0:T(8,128)(2,1)} %param.13, f32[3584]{0:T(1024)} %param.15, f32[256]{0:T(256)S(1)} %add_rsqrt_fusion.1), kind=kOutput, calls=%fused_computation.16 | convolution fusion | flops 1648066560 | bytes 9193984 | tf_op jit(solution)/shard_map/dot_general | solution.py:57
  15.7 2.6 %copy.23 = f32[256,896]{0,1:T(8,128)} copy(f32[256,896]{1,0:T(8,128)} %convolution_add_fusion) | data formatting | bytes 1835008 | tf_op jit(solution)/shard_map/add | solution.py:57
  18.3 2.2 reshape.119
  21.2 0.0 copy-done
  21.2 0.0 copy-done.1
  21.2 0.0 copy-done.7
  21.2 0.0 copy-done.8
  21.2 0.9 convolution_add_fusion.2
  22.1 0.1 broadcast_multiply_fusion
  22.2 1.1 fusion.18
  23.3 0.1 copy.26
  23.4 0.1 copy.22
  23.5 0.0 copy-start.4
  23.5 33.5 %all_gather.12 = bf16[2048,128]{0,1:T(8,128)(2,1)S(1)} all-gather(bf16[256,128]{0,1:T(8,128)(2,1)} %get-tuple-element.38), channel_id=1, replica_groups=mesh['seq'=8,'head'=4] {'seq'}, dimensions={0}, use_global_device_ids=true | all-gather | bytes 589824 | tf_op jit(solution)/shard_map/all_gather | solution.py:89
  57.0 1.9 fusion.10
  58.9 33.4 %all_gather.13 = bf16[2048,128]{1,0:T(8,128)(2,1)} all-gather(bf16[256,128]{1,0:T(8,128)(2,1)S(1)} %fusion.10), channel_id=1, replica_groups=mesh['seq'=8,'head'=4] {'seq'}, dimensions={0}, use_global_device_ids=true | all-gather | bytes 589824 | tf_op jit(solution)/shard_map/all_gather | solution.py:90
  92.3 0.9 slice_negate_fusion
  93.1 0.4 copy.24
  93.6 1.0 concatenate.28
  94.6 0.1 mul.130
  94.7 1.0 mul.131
  95.7 0.1 mul.133
  95.8 1.1 mul.134
  96.8 1.4 copy.25
  98.3 1.0 concatenate.29
  99.3 2.4 %fusion.13 = bf16[1792,128]{1,0:T(8,128)(2,1)S(1)} fusion(f32[1792,128]{1,0:T(8,128)} %mul.134, f32[1792,64]{1,0:T(8,128)} %concatenate.29, f32[1792,64]{1,0:T(8,128)} %concatenate.28, f32[1792,128]{1,0:T(8,128)S(1)} %copy-done.3, f32[1792,128]{1,0:T(8,128)} %mul.131), kind=kLoop, calls=%fused_computation.23 | loop fusion | flops 1376256 | bytes 4128768 | tf_op jit(solution)/shard_map/convert_element_type | solution.py:59
  101.7 22.9 %conditional.1 = (f32[1792]{0:T(1024)S(1)}, f32[1792,128]{1,0:T(8,128)S(1)}) conditional(s32[]{:T(128)} %convert_element_type.49, () %tuple.16, (s32[]{:T(128)}, bf16[1792,128]{1,0:T(8,128)(2,1)S(1)}, bf16[2048,128]{0,1:T(8,128)(2,1)S(1)}, bf16[2048,128]{1,0:T(8,128)(2,1)S(1)}) %tuple.32), branch_computations={%region_1.0_spmd, %region_2.5_spmd} | conditional | flops 1915748608 | bytes 46516244 | solution.py:99
  101.9 0.7 iota_compare_fusion
  102.6 7.3 %select_reduce_fusion = (f32[1792]{0:T(1024)S(1)}, f32[1792,2048]{1,0:T(8,128)}) fusion(pred[2048]{0:T(1024)(128)(4,1)S(1)} %iota_compare_fusion, bf16[1792,128]{1,0:T(8,128)(2,1)S(1)} %get-tuple-element.9, bf16[2048,128]{0,1:T(8,128)(2,1)S(1)} %get-tuple-element.28), kind=kOutput, calls=%fused_computation.1 | convolution fusion | flops 946862336 | bytes 15672320 | tf_op jit(solution)/shard_map/cond/branch_1_fun/dot_general | solution.py:32
  109.9 8.2 %fusion.1 = f32[1792]{0:T(1024)S(1)} fusion(f32[1792,2048]{1,0:T(8,128)} %get-tuple-element.31, f32[1792]{0:T(1024)S(1)} %broadcast_maximum_fusion, pred[2048]{0:T(1024)(128)(4,1)S(1)} %iota_compare_fusion), kind=kLoop, calls=%fused_computation.3 | loop fusion | flops 14678272 | bytes 14696448 | tf_op jit(solution)/shard_map/cond/branch_1_fun/reduce_sum | solution.py:79
  118.0 6.6 %fusion.2 = f32[1792,128]{1,0:T(8,128)S(1)} fusion(bf16[2048,128]{1,0:T(8,128)(2,1)S(1)} %get-tuple-element.11, f32[1792,2048]{1,0:T(8,128)} %get-tuple-element.31, f32[1792]{0:T(1024)S(1)} %broadcast_maximum_fusion, pred[2048]{0:T(1024)(128)(4,1)S(1)} %iota_compare_fusion), kind=kOutput, calls=%fused_computation.4 | convolution fusion | flops 954204160 | bytes 16131072 | tf_op jit(solution)/shard_map/cond/branch_1_fun/dot_general | solution.py:80
  124.6 0.3 divide_convert_fusion
  125.0 0.5 reshape.122
  125.4 6.1 %convolution_convert_fusion = bf16[256,3584]{1,0:T(8,128)(2,1)} fusion(bf16[256,896]{1,0:T(8,128)(2,1)S(1)} %reshape.122, bf16[896,3584]{1,0:T(8,128)(2,1)} %param.22), kind=kOutput, calls=%fused_computation.10 | convolution fusion | flops 1645084672 | bytes 8716288 | tf_op jit(solution)/shard_map/dot_general | solution.py:103
  131.6 4.0 %copy.29 = bf16[256,3584]{0,1:T(8,128)(2,1)} copy(bf16[256,3584]{1,0:T(8,128)(2,1)} %convolution_convert_fusion) | data formatting | bytes 3670016
  135.5 0.0 reduce-scatter.4.cloned.1.call-update
  135.6 30.9 %reduce-scatter.4.cloned.1.call-done = bf16[896,256]{1,0:T(8,128)(2,1)} async-done(((bf16[3584,256]{1,0:T(8,128)(2,1)}), bf16[896,256]{1,0:T(8,128)(2,1)}) %reduce-scatter.4.cloned.1.call-update) | async-done | bytes 458768
  166.5 1.3 copy.30
  167.8 0.2 multiply_reduce_fusion
  168.0 5.8 %psum.14 = f32[256]{0:T(256)S(1)} all-reduce(f32[256]{0:T(256)S(1)} %multiply_reduce_fusion), channel_id=1, replica_groups=mesh['seq'=8,'head'=4] {'head'}, use_global_device_ids=true, to_apply=%region_7.8 | all-reduce | flops 256 | bytes 2048 | tf_op jit(solution)/shard_map/psum | solution.py:112
  173.8 1.0 select_reduce_fusion.1
  174.8 30.8 %all-gather.1 = f32[8,1,896]{2,1,0:T(1,128)S(1)} all-gather(f32[1,1,896]{2,1,0:T(1,128)S(1)} %reshape.124), channel_id=2, replica_groups=mesh['seq'=8,'head'=4] {'seq'}, dimensions={0}, use_global_device_ids=true | all-gather | bytes 32256 | tf_op jit(solution)/shard_map/all_gather | solution.py:116
  205.6 0.6 multiply_reduce_fusion.1
  206.3 6.3 %psum.15 = f32[]{:T(128)} all-reduce(f32[]{:T(128)} %multiply_reduce_fusion.1), channel_id=1, replica_groups=mesh['seq'=8,'head'=4] {'head'}, use_global_device_ids=true, to_apply=%region_11.12 | all-reduce | flops 1 | bytes 8 | tf_op jit(solution)/shard_map/psum | solution.py:118
  213.2 0.6 broadcast_multiply_fusion.1
  (23 shorter events, 0.1 us)
Async XLA Ops:
  7.2 14.0 %copy-start = (bf16[3584,128]{1,0:T(8,128)(2,1)S(1)}, bf16[3584,128]{1,0:T(8,128)(2,1)}, u32[]{:S(2)}) copy-start(bf16[3584,128]{1,0:T(8,128)(2,1)} %param.18) | copy-start | bytes 2752516
  7.2 159.3 %reduce-scatter.4.cloned.1.call-start = ((), (), s32[]{:S(2)}) async-start(), calls=%async_computation.1 | async-start | bytes 2293760
  15.7 5.4 %copy-start.1 = (bf16[256,3584]{1,0:T(8,128)(2,1)S(1)}, bf16[256,3584]{1,0:T(8,128)(2,1)}, u32[]{:S(2)}) copy-start(bf16[256,3584]{1,0:T(8,128)(2,1)} %param.13) | copy-start | bytes 5505028
  15.7 5.5 %copy-start.7 = (f32[3584]{0:T(1024)S(1)}, f32[3584]{0:T(1024)}, u32[]{:S(2)}) copy-start(f32[3584]{0:T(1024)} %param.15) | copy-start | bytes 43012
  15.7 5.5 %copy-start.8 = (f32[128]{0:T(128)S(1)}, f32[128]{0:T(128)}, u32[]{:S(2)}) copy-start(f32[128]{0:T(128)} %param.19) | copy-start | bytes 1540
  18.3 38.7 %copy-start.9 = (f32[128]{0:T(128)S(1)}, f32[128]{0:T(128)}, u32[]{:S(2)}) copy-start(f32[128]{0:T(128)} %param.21) | copy-start | bytes 1540
  23.5 68.8 %copy-start.4 = (f32[256,896]{0,1:T(8,128)S(1)}, f32[256,896]{0,1:T(8,128)}, u32[]{:S(2)}) copy-start(f32[256,896]{0,1:T(8,128)} %copy.23) | copy-start | bytes 2752516
  95.7 3.6 %copy-start.3 = (f32[1792,128]{1,0:T(8,128)S(1)}, f32[1792,128]{1,0:T(8,128)}, u32[]{:S(2)}) copy-start(f32[1792,128]{1,0:T(8,128)} %reshape.119) | copy-start | bytes 2752516
  99.3 2.4 %copy-start.5 = (bf16[2048,128]{1,0:T(8,128)(2,1)S(1)}, bf16[2048,128]{1,0:T(8,128)(2,1)}, u32[]{:S(2)}) copy-start(bf16[2048,128]{1,0:T(8,128)(2,1)} %all_gather.13) | copy-start | bytes 1572868
  131.6 36.2 %copy-start.2 = (bf16[256,3584]{1,0:T(8,128)(2,1)S(1)}, bf16[256,3584]{1,0:T(8,128)(2,1)}, u32[]{:S(2)}) copy-start(bf16[256,3584]{1,0:T(8,128)(2,1)} %param.13) | copy-start | bytes 5505028
  131.6 42.2 %copy-start.6 = (f32[896]{0:T(1024)S(1)}, f32[896]{0:T(1024)}, u32[]{:S(2)}) copy-start(f32[896]{0:T(1024)} %param.23) | copy-start | bytes 10756
Sparse Core Ops, SparseCore 0:
  135.7 30.7 reduce-scatter.3
